TPU v7x, 16 devices: a 4x2x1 block of a 4x4x8 slice. The times are simulated.
16 devices in a mesh: dp: 2 (over y, z), tp: 8 (over x, core).
Axes of the slice: x: 4, y: 2, z: 1, core: 2. Of those that a mesh axis runs over, the one named last changes fastest.
The devices are a block of a 4x4x8 slice.
Arguments:
- hidden: bfloat16 [12, 6, 3072], P('dp'), parts along dimension 0
- draft_ids: int32 [12, 5], P('dp'), parts along dimension 0
- temperature: float32 [12], P('dp'), parts along dimension 0
- norm_gain: bfloat16 [3072], replicated
- head_weight: bfloat16 [128256, 3072], P('tp')
Outputs:
- output 1: float32 [12, 5], P('dp'), parts along dimension 0
- output 2: float32 [12, 6], P('dp'), parts along dimension 0
- output 3: float32 [12, 6], P('dp'), parts along dimension 0
There are 2 independent parts. A program takes and returns all parts, laid end to end along the dimension named above; an argument that names none is the same for every part.
All inputs are finite; a program needn't handle non-finite values.
Results may differ from a plain program's by a relative error of at most 0.001.
Values sent between devices are 32-bit elements.
A program may use at most 768 MiB of HBM per device.

v0:
```python
import jax
import jax.numpy as jnp
from jax import lax
from jax.sharding import PartitionSpec as P, NamedSharding

NORM_EPS = 1e-5


def solution(mesh):
    def local_step(hidden, draft_ids, value_a11, norm_gain, head_shard):
        draft_len = draft_ids.shape[1]
        hidden_f32 = hidden.astype(jnp.float32)
        mean_sq = jnp.mean(hidden_f32 * hidden_f32, axis=-1, keepdims=True)
        normed = (hidden_f32 * lax.rsqrt(mean_sq + NORM_EPS) * norm_gain.astype(jnp.float32)).astype(jnp.bfloat16)
        shard_logits = jnp.einsum("bpd,vd->bpv", normed, head_shard, preferred_element_type=jnp.float32)
        shard_logits = shard_logits / value_a11[:, None, None]
        logits = lax.all_gather(shard_logits, "tp", axis=2, tiled=True)
        row_max = jnp.max(logits, axis=-1, keepdims=True)
        shifted = jnp.exp(logits - row_max)
        total = jnp.sum(shifted, axis=-1)
        weighted = jnp.sum(shifted * logits, axis=-1)
        log_norm = row_max[..., 0] + jnp.log(total)
        entropy = log_norm - weighted / total
        picked = jnp.take_along_axis(logits[:, :draft_len], draft_ids[:, :, None], axis=2)[..., 0]
        return picked - log_norm[:, :draft_len], log_norm, entropy

    return jax.shard_map(
        local_step,
        mesh=mesh,
        in_specs=(P("dp", None, None), P("dp", None), P("dp"), P(None), P("tp", None)),
        out_specs=(P("dp", None), P("dp", None), P("dp", None)),
        check_vma=False,
    )
```

profile of v0, /device:TPU:113, one launch (start us, length us, event | category | flops | bytes accessed | tf_op | source)
XLA Modules:
  0.0 2898.7 jit_solution(13692356504559391065)
XLA Ops:
  7.2 0.1 all-gather.2.cloned.1.call-start
  7.2 0.7 convert_element_type.10
  7.9 1.1 fusion.6
  9.1 0.0 copy-start.2
  9.1 37.6 %fusion.3 = f32[6,6,16032]{2,1,0:T(8,128)S(1)} fusion(bf16[16032,3072]{1,0:T(8,128)(2,1)} %param.9, f32[6]{0:T(128)} %param.7, bf16[6,6,3072]{2,1,0:T(8,128)(2,1)} %param.5, f32[3072]{0:T(1024)S(1)} %convert_element_type.10, f32[6,6]{1,0:T(8,128)S(1)} %add_rsqrt_fusion), kind=kOutput, calls=%fused_computation.6 | convolution fusion | flops 3547041280 | bytes 101042856 | tf_op jit(solution)/shard_map/bpd,vd->bpv/dot_general | solution.py:15
  46.7 30.3 %copy.12 = f32[6,6,16032]{1,0,2:T(8,128)} copy(f32[6,6,16032]{2,1,0:T(8,128)S(1)} %fusion.3) | data formatting | bytes 4617216 | tf_op jit(solution)/shard_map/div | solution.py:16
  77.0 0.1 all-gather.2.cloned.1.call-update
  77.1 0.0 copy-done.2
  77.2 0.1 copy.14
  77.3 0.1 copy.15
  77.4 0.6 reshape.42
  78.0 2220.1 %all-gather.2.cloned.1.call-done = f32[6,6,128256]{1,0,2:T(8,128)} async-done(((f32[6,6,16032]{1,0,2:T(8,128)}), f32[6,6,128256]{1,0,2:T(8,128)}) %all-gather.2.cloned.1.call-update) | async-done | bytes 18468880 | tf_op jit(solution)/shard_map/all_gather | solution.py:17
  2298.1 0.0 copy-start
  2298.1 257.8 %copy.16 = f32[6,5,128256]{2,1,0:T(8,128)} copy(f32[6,5,128256]{1,0,2:T(8,128)} %bitcast.10) | data formatting | bytes 30781440
  2555.9 0.0 copy-done
  2555.9 1.8 gather_fusion
  2557.6 0.7 gather.7
  2558.3 156.8 %reduce_max.9 = f32[6,6]{1,0:T(8,128)S(1)} reduce(f32[6,6,128256]{1,0,2:T(8,128)} %all-gather.2.cloned.1.call-done, f32[]{:T(128)} %constant.24.clone.1), dimensions={2}, to_apply=%region_1.0 | reduce | flops 4617180 | bytes 18469012 | tf_op jit(solution)/shard_map/reduce_max | solution.py:18
  2715.1 0.0 copy-start.3
  2715.1 0.0 copy-start.4
  2715.1 175.5 %multiply_reduce_fusion = (f32[6,6]{1,0:T(8,128)S(1)}, f32[6,6]{1,0:T(8,128)S(1)}) fusion(f32[6,6,128256]{1,0,2:T(8,128)} %all-gather.2.cloned.1.call-done, f32[6,6]{1,0:T(8,128)S(1)} %reduce_max.9), kind=kLoop, calls=%fused_computation.1 | loop fusion | flops 18468792 | bytes 18469296 | tf_op jit(solution)/shard_map/reduce_sum | solution.py:21
  2890.6 0.6 divide_subtract_fusion
  2891.2 0.0 copy-start.1
  2891.2 0.0 copy-done.3
  2891.2 0.0 copy-done.4
  2891.2 0.6 slice_subtract_fusion
  2891.8 0.0 copy-done.1
  (6 shorter events, 0.0 us)
Async XLA Ops:
  7.2 2290.9 %all-gather.2.cloned.1.call-start = ((), (), s32[]{:S(2)}) async-start(), calls=%async_computation | async-start | bytes 591003648 | tf_op jit(solution)/shard_map/all_gather | solution.py:17
  9.1 68.0 %copy-start.2 = (s32[6,5]{1,0:T(8,128)S(1)}, s32[6,5]{1,0:T(8,128)}, u32[]{:S(2)}) copy-start(s32[6,5]{1,0:T(8,128)} %param.6) | copy-start | bytes 364
  2298.1 257.8 %copy-start = (s32[30]{0:T(128)S(1)}, s32[30]{0:T(128)}, u32[]{:S(2)}) copy-start(s32[30]{0:T(128)} %reshape.42) | copy-start | bytes 364
  2715.1 176.1 %copy-start.3 = (s32[6,5]{1,0:T(8,128)S(1)}, s32[6,5]{1,0:T(8,128)}, u32[]{:S(2)}) copy-start(s32[6,5]{1,0:T(8,128)} %param.6) | copy-start | bytes 364
  2715.1 176.1 %copy-start.4 = (f32[6,5]{1,0:T(8,128)S(1)}, f32[6,5]{1,0:T(8,128)}, u32[]{:S(2)}) copy-start(f32[6,5]{1,0:T(8,128)} %gather.7) | copy-start | bytes 364
  2891.2 0.6 copy-start.1
Sparse Core Ops, SparseCore 0:
  77.2 2220.7 all-gather.1
where the time goes:
time: 2900 us
  waiting for transfers between devices  2220 us (77%)
  other arithmetic  335 us (12%)
  local copies, waits for them, and re-layouts  291 us (10%)
  matrix products  37.6 us (1%)
    all_gather x1, waiting for transfers between devices, local_step(): logits = lax.all_gather(shard_logits, 'tp', axis=2, tiled=True)  2220 us
    unnamed x13, local copies, waits for them, and re-layouts  258 us
    reduce_sum x1, other arithmetic, local_step(): weighted = jnp.sum(shifted * logits, axis=-1)  175 us
    reduce_max x1, other arithmetic, local_step(): row_max = jnp.max(logits, axis=-1, keepdims=True)  157 us
  transfers between devices with their start and end apart: 1, of which 1 were waited for; matrix products, arithmetic and copies ran while one was open for 0% of the time, Pallas kernels for 0%

commit v1 on v0

v1 whole, which is shorter than its diff:
```python
import functools

import jax
import jax.numpy as jnp
from jax import lax
from jax.experimental import pallas as pl
from jax.experimental.pallas import tpu as pltpu
from jax.sharding import PartitionSpec as P

NORM_EPS = 1e-5
MESH = pl.DeviceIdType.MESH
LOG2E = 1.4426950408889634
LN2 = 0.6931471805599453
LOW = -1e30
CHUNK = 1024
SLOTS = 6
OTHER = 64
PAIRED = True
OWN_CHUNKS = 4


def kernel(
    tp_size, n_own, n_all, last_rows, first_rows, share_rows,
    hidden_hbm, draft_ref, temp_ref, gain_hbm, w_hbm,
    lp_ref, lse_ref, ent_ref,
    hv, gv, gs, gr, g2, buf, zs, vecs, ids_v, vecs_r, stats, msg, inbox,
    in_sem, w_sem, k_sem, g_send, g_recv, p_send, p_recv, f_send, f_recv, s_send, s_recv,
):
    dp, tp = lax.axis_index("dp"), lax.axis_index("tp")
    half = lax.rem(dp, 2)
    mate = dp + 1 - 2 * half
    core = lax.rem(tp, 2)
    twin = tp + 1 - 2 * core
    shard_rows, dim = w_hbm.shape
    batch, width = hidden_hbm.shape[:2]
    draft_len = draft_ref.shape[1]
    hd = dim // 2
    pad_rows = gs.shape[1]

    def peer(o, other):
        return (mate if other else dp, lax.rem(tp + o, tp_size))

    peers = [(o, False) for o in range(1, tp_size)]
    if PAIRED:
        peers += [(o, True) for o in range(tp_size)]

    barrier = pltpu.get_barrier_semaphore()
    for o, other in peers:
        pl.semaphore_signal(barrier, inc=1, device_id=peer(o, other), device_id_type=MESH)

    h_copy = pltpu.make_async_copy(hidden_hbm, hv, in_sem.at[0])
    gain_copy = pltpu.make_async_copy(gain_hbm, gv, in_sem.at[1])
    h_copy.start()
    gain_copy.start()

    own_rows = first_rows + n_own * CHUNK
    shared_base = own_rows + half * share_rows if PAIRED else own_rows

    def offset(j, late):
        if late:
            return shared_base + (j - 1 - n_own) * CHUNK
        return first_rows + (j - 1) * CHUNK

    def w_copy(j, late, rows=CHUNK):
        row = pl.multiple_of(offset(j, late), 16)
        slot = lax.rem(j, SLOTS)
        return pltpu.make_async_copy(w_hbm.at[pl.ds(row, rows)], buf.at[slot, pl.ds(0, rows)], w_sem.at[slot])

    def start_last():
        j = n_all - 1
        row = pl.multiple_of(offset(j, True), 16)
        for k in range(k_parts):
            last_copy(row, k).start()

    k_parts = k_sem.shape[0]
    k_width = dim // k_parts

    def last_copy(row, k):
        return pltpu.make_async_copy(
            w_hbm.at[pl.ds(row, last_rows), pl.ds(k * k_width, k_width)],
            buf.at[(n_all - 1) % SLOTS, pl.ds(0, last_rows), pl.ds(k * k_width, k_width)],
            k_sem.at[k],
        )

    first_copy = pltpu.make_async_copy(w_hbm.at[pl.ds(0, first_rows)], buf.at[0, pl.ds(0, first_rows)], w_sem.at[0])
    first_copy.start()
    for j in range(1, SLOTS):
        w_copy(j, j > n_own).start()

    lane = lax.broadcasted_iota(jnp.int32, (1, 128), 1)
    scale = jnp.zeros((1, 128), jnp.float32)
    ids = jnp.full((1, 128), -1, jnp.int32)
    for b in range(batch):
        inside = (lane >= b * width) & (lane < (b + 1) * width)
        scale = jnp.where(inside, temp_ref[b], scale)
        for i in range(draft_len):
            ids = jnp.where(lane == b * width + i, draft_ref[b, i], ids)
    scale = jnp.where(lane < batch * width, LOG2E / jnp.where(scale == 0.0, 1.0, scale), 0.0)
    vecs[...] = jnp.zeros_like(vecs)
    vecs[0:1, :] = scale
    vecs[1:2, :] = ids.astype(jnp.float32)
    ids_v[...] = jnp.broadcast_to(ids, (8, 128))
    stats[0] = jnp.full((8, 128), LOW, jnp.float32)
    stats[1] = jnp.zeros((8, 128), jnp.float32)
    stats[2] = jnp.zeros((8, 128), jnp.float32)
    stats[3] = jnp.zeros((8, 128), jnp.float32)
    g2[...] = jnp.zeros_like(g2)

    h_copy.wait()
    gain_copy.wait()
    gain = gv[...].astype(jnp.float32)
    for c in range(2):
        gs[c, batch * width :, :] = jnp.zeros((pad_rows - batch * width, hd), jnp.float32)
    for b in range(batch):
        hb = hv[b].astype(jnp.float32)
        mean_sq = jnp.sum(hb * hb, axis=-1, keepdims=True) * (1.0 / dim)
        g = (hb * lax.rsqrt(mean_sq + NORM_EPS) * gain).astype(jnp.bfloat16).astype(jnp.float32)
        for c in range(2):
            gs[c, b * width : (b + 1) * width, :] = g[:, c * hd : (c + 1) * hd]
    for c in range(2):
        g2[0:pad_rows, c * hd : (c + 1) * hd] = gs[c].astype(jnp.bfloat16)

    pl.semaphore_wait(barrier, len(peers))

    g_copy = pltpu.make_async_remote_copy(
        src_ref=gs.at[core], dst_ref=gr.at[core], send_sem=g_send, recv_sem=g_recv,
        device_id=(mate, tp), device_id_type=MESH)
    p_copy = pltpu.make_async_remote_copy(
        src_ref=vecs, dst_ref=vecs_r, send_sem=p_send, recv_sem=p_recv,
        device_id=(mate, tp), device_id_type=MESH)
    f_copy = pltpu.make_async_remote_copy(
        src_ref=gr.at[core], dst_ref=gr.at[core], send_sem=f_send, recv_sem=f_recv.at[core],
        device_id=(dp, twin), device_id_type=MESH)
    f_wait = pltpu.make_async_remote_copy(
        src_ref=gr.at[1 - core], dst_ref=gr.at[1 - core], send_sem=f_send, recv_sem=f_recv.at[1 - core],
        device_id=(dp, twin), device_id_type=MESH)
    if PAIRED:
        g_copy.start()
        p_copy.start()

    def forward():
        g_copy.wait_recv()
        f_copy.start()

    def join():
        f_wait.wait_recv()
        for c in range(2):
            g2[OTHER : OTHER + pad_rows, c * hd : (c + 1) * hd] = gr[c].astype(jnp.bfloat16)

    def join_lanes():
        p_copy.wait_recv()
        theirs = lane >= OTHER
        v = pltpu.roll(vecs_r[...], OTHER, 1)
        scale_all[...] = jnp.where(theirs, v[0:1], scale_all[...])
        ids_v[...] = jnp.where(theirs, jnp.broadcast_to(v[1:2].astype(jnp.int32), (8, 128)), ids_v[...])
        stats[0] = jnp.where(theirs, LOW, stats[0])
        for r in range(1, 4):
            stats[r] = jnp.where(theirs, 0.0, stats[r])

    scale_all = msg.at[1]
    scale_all[...] = jnp.broadcast_to(scale, (8, 128))

    def epilogue(z, base):
        rows = z.shape[0]
        z = z.reshape(rows // 8, 8, 128) * scale_all[...][None]
        old = stats[0]
        new = jnp.maximum(old, jnp.max(z, axis=0))
        e = jnp.exp2(z - new[None])
        fix = jnp.exp2(old - new)
        stats[0] = new
        stats[1] = stats[1] * fix + jnp.sum(e, axis=0)
        stats[2] = stats[2] * fix + jnp.sum(e * z, axis=0)
        row = lax.broadcasted_iota(jnp.int32, z.shape, 0) * 8 + lax.broadcasted_iota(jnp.int32, z.shape, 1)
        hit = row == (ids_v[...] - (tp * shard_rows + base))[None]
        stats[3] = stats[3] + jnp.sum(jnp.where(hit, z, 0.0), axis=0)

    def product(slot, rows, k0=0, k1=dim):
        part = rows // 2
        return [
            lax.dot_general(
                buf[slot, q * part : (q + 1) * part, k0:k1], g2[:, k0:k1],
                (((1,), (1,)), ((), ())), preferred_element_type=jnp.float32)
            for q in range(2)
        ]

    def put(par, parts):
        rows = parts[0].shape[0]
        for q in range(2):
            zs[par, q * rows : (q + 1) * rows] = parts[q]

    def drain(par, base):
        part = CHUNK // 2
        for q in range(2):
            epilogue(zs[par, q * part : (q + 1) * part], base + q * part)

    def start_chunk(j):
        if j < n_all - 1:
            w_copy(jnp.int32(j), True).start()
        elif j == n_all - 1:
            start_last()

    first_copy.wait()
    parts = product(0, first_rows)
    start_chunk(SLOTS)
    for q in range(2):
        epilogue(parts[q], q * (first_rows // 2))

    late0 = n_own + 1
    forward_at = late0 - 1

    def base_of(j):
        early = first_rows + (j - 1) * CHUNK
        return early + jnp.where(j >= late0, shared_base - own_rows, 0)

    def step(j, par):
        slot = lax.rem(j, SLOTS)
        if PAIRED and forward_at % 2 == par:
            pl.when(j == forward_at)(forward)
        if PAIRED and late0 % 2 == par:
            pl.when(j == late0)(join)
        pltpu.make_async_copy(w_hbm.at[pl.ds(0, CHUNK)], buf.at[slot], w_sem.at[slot]).wait()
        parts = product(slot, CHUNK)

        if isinstance(j, int):
            put(par, parts)
            start_chunk(j + SLOTS)
            return
        drain(1 - par, base_of(j - 1))
        put(par, parts)
        if PAIRED and late0 % 2 == par:
            pl.when(j == late0)(join_lanes)

        @pl.when(j + SLOTS < n_all - 1)
        def _():
            w_copy(j + SLOTS, True).start()

        @pl.when(j + SLOTS == n_all - 1)
        def _():
            start_last()

    step(1, 1)
    n_loop = n_all - 3

    def body(i, carry):
        step(2 + 2 * i, 0)
        step(3 + 2 * i, 1)
        return carry

    lax.fori_loop(0, n_loop // 2, body, 0)
    if n_loop % 2:
        step(jnp.int32(n_all - 2), 0)

    row = pl.multiple_of(offset(n_all - 1, True), 16)
    parts = None
    for k in range(k_parts):
        last_copy(row, k).wait()
        more = product((n_all - 1) % SLOTS, last_rows, k * k_width, (k + 1) * k_width)
        parts = more if parts is None else [x + y for x, y in zip(parts, more)]
        if k == 0:
            drain((n_all - 2) % 2, base_of(n_all - 2))
    for q in range(2):
        epilogue(parts[q], row + q * (last_rows // 2))

    m8 = stats[0]
    m1 = jnp.max(m8, axis=0, keepdims=True)
    w8 = jnp.exp2(m8 - m1)
    out = msg.at[0]
    out[4:8, :] = jnp.zeros((4, 128), jnp.float32)
    out[0:1, :] = m1
    out[1:2, :] = jnp.sum(stats[1] * w8, axis=0, keepdims=True)
    out[2:3, :] = jnp.sum(stats[2] * w8, axis=0, keepdims=True)
    out[3:4, :] = jnp.sum(stats[3], axis=0, keepdims=True)

    def s_copy(o, other, source):
        i = 1 if other else 0
        return pltpu.make_async_remote_copy(
            src_ref=msg.at[0], dst_ref=inbox.at[i, source], send_sem=s_send.at[i, o], recv_sem=s_recv.at[i, source],
            device_id=peer(o, other), device_id_type=MESH)

    for o, other in peers:
        s_copy(o, other, tp).start()
    inbox[0, tp] = msg[0]
    for o, other in peers:
        s_copy(o, other, lax.rem(tp - o + tp_size, tp_size)).wait_recv()

    def combine(x):
        m = jnp.max(x[:, 0:1, :], axis=0)
        r = lax.broadcasted_iota(jnp.int32, x.shape, 1)
        weight = jnp.exp2(x[:, 0:1, :] - m[None])
        s = jnp.sum(jnp.where((r == 1) | (r == 2), x * weight, x), axis=0)
        return m, s

    m, s = combine(inbox[0])
    if PAIRED:
        m2, s2 = combine(inbox[1])
        m2 = pltpu.roll(jnp.broadcast_to(m2, (8, 128)), OTHER, 1)[0:1]
        s2 = pltpu.roll(s2, OTHER, 1)
        top = jnp.maximum(m, m2)
        r = lax.broadcasted_iota(jnp.int32, s.shape, 0)
        ours, theirs = jnp.exp2(m - top), jnp.exp2(m2 - top)
        scaled = (r == 1) | (r == 2)
        s = jnp.where(scaled, s * ours, s) + jnp.where(scaled, s2 * theirs, s2)
        m = top
    lse = m * LN2 + jnp.log(s[1:2])
    ent = lse - LN2 * (s[2:3] / s[1:2])
    lp = LN2 * s[3:4] - lse

    if PAIRED:
        p_copy.wait_send()
    vecs[0:1, :] = lse
    vecs[1:2, :] = ent
    vecs[2:3, :] = lp
    for b in range(batch):
        line = pltpu.roll(vecs[...], (128 - b * width) % 128, 1)
        lse_ref[b : b + 1, :] = line[0:1, :width]
        ent_ref[b : b + 1, :] = line[1:2, :width]
        lp_ref[b : b + 1, :] = line[2:3, :draft_len]

    for o, other in peers:
        s_copy(o, other, tp).wait_send()
    if PAIRED:
        g_copy.wait_send()
        f_copy.wait_send()


def solution(mesh):
    tp_size = mesh.shape["tp"]

    def local_step(hidden, draft_ids, temperature, norm_gain, head_shard):
        batch, width, dim = hidden.shape
        shard_rows = head_shard.shape[0]
        first_rows = shard_rows % CHUNK
        full = shard_rows // CHUNK
        if PAIRED:
            n_own = OWN_CHUNKS
            share_rows = (shard_rows - first_rows - n_own * CHUNK) // 2
            n_late = -(-share_rows // CHUNK)
            last_rows = share_rows - (n_late - 1) * CHUNK
            n_all = 1 + n_own + n_late
        else:
            n_own, share_rows, n_all, last_rows = 0, 0, 1 + full, CHUNK
        pad_rows = -(-batch * width // 8) * 8
        vmem, dma = pltpu.VMEM, pltpu.SemaphoreType.DMA
        f32, bf16 = jnp.float32, jnp.bfloat16
        any_space = pl.BlockSpec(memory_space=pltpu.HBM)
        smem = pl.BlockSpec(memory_space=pltpu.SMEM)
        out = pl.BlockSpec(memory_space=pltpu.VMEM)
        return pl.pallas_call(
            functools.partial(kernel, tp_size, n_own, n_all, last_rows, first_rows, share_rows),
            out_shape=(
                jax.ShapeDtypeStruct(draft_ids.shape, f32),
                jax.ShapeDtypeStruct((batch, width), f32),
                jax.ShapeDtypeStruct((batch, width), f32),
            ),
            in_specs=[any_space, smem, smem, any_space, any_space],
            out_specs=(out, out, out),
            scratch_shapes=[
                vmem(hidden.shape, bf16),
                vmem((1, dim), bf16),
                vmem((2, pad_rows, dim // 2), f32),
                vmem((2, pad_rows, dim // 2), f32),
                vmem((128, dim), bf16),
                vmem((SLOTS, CHUNK, dim), bf16),
                vmem((2, CHUNK, 128), f32),
                vmem((8, 128), f32),
                vmem((8, 128), jnp.int32),
                vmem((8, 128), f32),
                vmem((4, 8, 128), f32),
                vmem((2, 8, 128), f32),
                vmem((2, tp_size, 8, 128), f32),
                dma((2,)), dma((SLOTS,)), dma((4,)),
                dma, dma, dma, dma, dma, dma((2,)),
                dma((2, tp_size)), dma((2, tp_size)),
            ],
            compiler_params=pltpu.CompilerParams(
                collective_id=0, has_side_effects=True, vmem_limit_bytes=60 * 2**20),
        )(hidden, draft_ids, temperature, norm_gain.reshape(1, dim), head_shard)

    return jax.shard_map(
        local_step,
        mesh=mesh,
        in_specs=(P("dp", None, None), P("dp", None), P("dp"), P(None), P("tp", None)),
        out_specs=(P("dp", None), P("dp", None), P("dp", None)),
        check_vma=False,
    )
```

time: 2900 us -> 47 us (0.02)
  waiting for transfers between devices: 2220 us -> 0 us
  other arithmetic: 335 us -> 0 us
  local copies, waits for them, and re-layouts: 291 us -> 5.1 us
  Pallas kernels: 0 us -> 40.9 us
  matrix products: 37.6 us -> 0 us
    all_gather x1 -> x0, waiting for transfers between devices: 2220 us -> none  [local_step(): logits = lax.all_gather(shard_logits, 'tp', axis=2, tiled=True)]
    unnamed x13 -> x3, local copies, waits for them, and re-layouts: 258 us -> 3.8 us
    reduce_sum x2 -> x0, other arithmetic: 177 us -> none  [the longest x1 175 us: local_step(): weighted = jnp.sum(shifted * logits, axis=-1)]
    reduce_max x1 -> x0, other arithmetic: 157 us -> none  [local_step(): row_max = jnp.max(logits, axis=-1, keepdims=True)]
    pallas_call x0 -> x1, Pallas kernels: none -> 40.9 us  [local_step(): pl.pallas_call(functools.partial(kernel, tp_size, n_own, n_all, last_rows...]
    dot_general x1 -> x0, matrix products: 37.6 us -> none  [local_step(): jnp.einsum('bpd,vd->bpv', normed, head_shard, preferred_element_type=jnp....]
    div x1 -> x0, local copies, waits for them, and re-layouts: 30.3 us -> none  [local_step(): shard_logits = shard_logits / value_a11[:, None, None]]
  transfers between devices with their start and end apart: 1 -> 0, of which waited for: 1 -> 0; matrix products, arithmetic and copies ran while one was open for 0% -> 0% of each run, Pallas kernels for 0% -> 0%
where the time goes in v1:
time: 47 us; the launch traced here: 46.6 us
  Pallas kernels  40.9 us (87%)
  local copies, waits for them, and re-layouts  5.1 us (11%)
  between operations  0.64 us (1%)
    pallas_call x1, Pallas kernels, local_step(): pl.pallas_call(functools.partial(kernel, tp_size, n_own, n_all, last_rows...  40.9 us
    unnamed x3, local copies, waits for them, and re-layouts  3.8 us
    reshape x1, local copies, waits for them, and re-layouts, local_step(): norm_gain.reshape(1, dim)  1.3 us

profile of v1, /device:TPU:113, one launch (start us, length us, event | category | flops | bytes accessed | tf_op | source)
XLA Modules:
  0.0 46.6 jit_solution(912341965868612411)
XLA Ops:
  0.6 1.3 %reshape.9.gain_hbm = bf16[1,3072]{1,0:T(2,128)(2,1)} reshape(bf16[3072]{0:T(1024)(128)(2,1)} %param.8) | data formatting | bytes 12288 | tf_op jit(solution)/shard_map/reshape | solution.py:377
  1.9 40.9 %shard_map.76 = (f32[6,5]{1,0:T(8,128)}, f32[6,6]{1,0:T(8,128)}, f32[6,6]{1,0:T(8,128)}) custom-call(bf16[6,6,3072]{2,1,0:T(8,128)(2,1)} %hidden_hbm.1, s32[6,5]{1,0:T(8,128)} %draft_ref.1, f32[6]{0:T(128)} %temp_ref.1, bf16[1,3072]{1,0:T(2,128)(2,1)} %reshape.9.gain_hbm, bf16[16032,3072]{1,0:T(8,128)(2,1)} %w_hbm.1), custom_call_target="tpu_custom_call" | custom-call | tf_op jit(solution)/shard_map/pallas_call | solution.py:348
  42.8 1.3 %copy.11 = f32[6,5]{1,0:T(8,128)} copy(f32[6,5]{1,0:T(8,128)} %get-tuple-element.6) | data formatting | bytes 240
  44.1 1.3 %copy.12 = f32[6,6]{1,0:T(8,128)} copy(f32[6,6]{1,0:T(8,128)} %get-tuple-element.7) | data formatting | bytes 288
  45.3 1.3 %copy.13 = f32[6,6]{1,0:T(8,128)} copy(f32[6,6]{1,0:T(8,128)} %get-tuple-element.8) | data formatting | bytes 288

commit v2 on v1

--- a/solution.py
+++ b/solution.py
@@ -21,9 +21,9 @@
 
 def kernel(
     tp_size, n_own, n_all, last_rows, first_rows, share_rows,
-    hidden_hbm, draft_ref, temp_ref, gain_hbm, w_hbm,
-    lp_ref, lse_ref, ent_ref,
-    hv, gv, gs, gr, g2, buf, zs, vecs, ids_v, vecs_r, stats, msg, inbox,
+    hidden_hbm, draft_hbm, temp_hbm, gain_hbm, w_hbm,
+    out_ref,
+    draft_ref, temp_ref, hv, gv, gs, gr, g2, buf, zs, vecs, ids_v, vecs_r, stats, msg, inbox,
     in_sem, w_sem, k_sem, g_send, g_recv, p_send, p_recv, f_send, f_recv, s_send, s_recv,
 ):
     dp, tp = lax.axis_index("dp"), lax.axis_index("tp")
@@ -33,16 +33,16 @@
     twin = tp + 1 - 2 * core
     shard_rows, dim = w_hbm.shape
     batch, width = hidden_hbm.shape[:2]
-    draft_len = draft_ref.shape[1]
+    draft_len = draft_hbm.shape[1]
     hd = dim // 2
     pad_rows = gs.shape[1]
 
     def peer(o, other):
         return (mate if other else dp, lax.rem(tp + o, tp_size))
 
-    peers = [(o, False) for o in range(1, tp_size)]
-    if PAIRED:
-        peers += [(o, True) for o in range(tp_size)]
+    far_first = sorted(range(tp_size), key=lambda o: -min(o, tp_size - o))
+    peers = [(o, True) for o in far_first] if PAIRED else []
+    peers += [(o, False) for o in far_first if o]
 
     barrier = pltpu.get_barrier_semaphore()
     for o, other in peers:
@@ -50,8 +50,12 @@
 
     h_copy = pltpu.make_async_copy(hidden_hbm, hv, in_sem.at[0])
     gain_copy = pltpu.make_async_copy(gain_hbm, gv, in_sem.at[1])
+    draft_copy = pltpu.make_async_copy(draft_hbm, draft_ref, in_sem.at[2])
+    temp_copy = pltpu.make_async_copy(temp_hbm, temp_ref, in_sem.at[3])
     h_copy.start()
     gain_copy.start()
+    draft_copy.start()
+    temp_copy.start()
 
     own_rows = first_rows + n_own * CHUNK
     shared_base = own_rows + half * share_rows if PAIRED else own_rows
@@ -70,7 +74,7 @@
         j = n_all - 1
         row = pl.multiple_of(offset(j, True), 16)
         for k in range(k_parts):
-            last_copy(row, k).start()
+            last_copy(row, k).start(priority=1)
 
     k_parts = k_sem.shape[0]
     k_width = dim // k_parts
@@ -83,10 +87,12 @@
         )
 
     first_copy = pltpu.make_async_copy(w_hbm.at[pl.ds(0, first_rows)], buf.at[0, pl.ds(0, first_rows)], w_sem.at[0])
-    first_copy.start()
+    first_copy.start(priority=1)
     for j in range(1, SLOTS):
-        w_copy(j, j > n_own).start()
-
+        w_copy(j, j > n_own).start(priority=1)
+
+    draft_copy.wait()
+    temp_copy.wait()
     lane = lax.broadcasted_iota(jnp.int32, (1, 128), 1)
     scale = jnp.zeros((1, 128), jnp.float32)
     ids = jnp.full((1, 128), -1, jnp.int32)
@@ -108,7 +114,7 @@
 
     h_copy.wait()
     gain_copy.wait()
-    gain = gv[...].astype(jnp.float32)
+    gain = gv[...].astype(jnp.float32).reshape(1, dim)
     for c in range(2):
         gs[c, batch * width :, :] = jnp.zeros((pad_rows - batch * width, hd), jnp.float32)
     for b in range(batch):
@@ -119,8 +125,6 @@
             gs[c, b * width : (b + 1) * width, :] = g[:, c * hd : (c + 1) * hd]
     for c in range(2):
         g2[0:pad_rows, c * hd : (c + 1) * hd] = gs[c].astype(jnp.bfloat16)
-
-    pl.semaphore_wait(barrier, len(peers))
 
     g_copy = pltpu.make_async_remote_copy(
         src_ref=gs.at[core], dst_ref=gr.at[core], send_sem=g_send, recv_sem=g_recv,
@@ -134,10 +138,6 @@
     f_wait = pltpu.make_async_remote_copy(
         src_ref=gr.at[1 - core], dst_ref=gr.at[1 - core], send_sem=f_send, recv_sem=f_recv.at[1 - core],
         device_id=(dp, twin), device_id_type=MESH)
-    if PAIRED:
-        g_copy.start()
-        p_copy.start()
-
     def forward():
         g_copy.wait_recv()
         f_copy.start()
@@ -195,11 +195,15 @@
 
     def start_chunk(j):
         if j < n_all - 1:
-            w_copy(jnp.int32(j), True).start()
+            w_copy(jnp.int32(j), True).start(priority=1)
         elif j == n_all - 1:
             start_last()
 
     first_copy.wait()
+    pl.semaphore_wait(barrier, len(peers))
+    if PAIRED:
+        g_copy.start()
+        p_copy.start()
     parts = product(0, first_rows)
     start_chunk(SLOTS)
     for q in range(2):
@@ -232,7 +236,7 @@
 
         @pl.when(j + SLOTS < n_all - 1)
         def _():
-            w_copy(j + SLOTS, True).start()
+            w_copy(j + SLOTS, True).start(priority=1)
 
         @pl.when(j + SLOTS == n_all - 1)
         def _():
@@ -310,17 +314,22 @@
     vecs[0:1, :] = lse
     vecs[1:2, :] = ent
     vecs[2:3, :] = lp
-    for b in range(batch):
-        line = pltpu.roll(vecs[...], (128 - b * width) % 128, 1)
-        lse_ref[b : b + 1, :] = line[0:1, :width]
-        ent_ref[b : b + 1, :] = line[1:2, :width]
-        lp_ref[b : b + 1, :] = line[2:3, :draft_len]
+    out_ref[...] = vecs[...]
 
     for o, other in peers:
         s_copy(o, other, tp).wait_send()
     if PAIRED:
         g_copy.wait_send()
         f_copy.wait_send()
+
+
+def unpack(lines_ref, lp_ref, lse_ref, ent_ref):
+    batch, width = lse_ref.shape
+    for b in range(batch):
+        line = pltpu.roll(lines_ref[...], (128 - b * width) % 128, 1)
+        lse_ref[b : b + 1, :] = line[0:1, :width]
+        ent_ref[b : b + 1, :] = line[1:2, :width]
+        lp_ref[b : b + 1, :] = line[2:3, : lp_ref.shape[1]]
 
 
 def solution(mesh):
@@ -343,20 +352,17 @@
         vmem, dma = pltpu.VMEM, pltpu.SemaphoreType.DMA
         f32, bf16 = jnp.float32, jnp.bfloat16
         any_space = pl.BlockSpec(memory_space=pltpu.HBM)
-        smem = pl.BlockSpec(memory_space=pltpu.SMEM)
         out = pl.BlockSpec(memory_space=pltpu.VMEM)
-        return pl.pallas_call(
+        lines = pl.pallas_call(
             functools.partial(kernel, tp_size, n_own, n_all, last_rows, first_rows, share_rows),
-            out_shape=(
-                jax.ShapeDtypeStruct(draft_ids.shape, f32),
-                jax.ShapeDtypeStruct((batch, width), f32),
-                jax.ShapeDtypeStruct((batch, width), f32),
-            ),
-            in_specs=[any_space, smem, smem, any_space, any_space],
-            out_specs=(out, out, out),
+            out_shape=pltpu.VMEM((8, 128), f32),
+            in_specs=[any_space] * 5,
+            out_specs=out,
             scratch_shapes=[
+                pltpu.SMEM(draft_ids.shape, jnp.int32),
+                pltpu.SMEM(temperature.shape, f32),
                 vmem(hidden.shape, bf16),
-                vmem((1, dim), bf16),
+                vmem((dim,), bf16),
                 vmem((2, pad_rows, dim // 2), f32),
                 vmem((2, pad_rows, dim // 2), f32),
                 vmem((128, dim), bf16),
@@ -368,13 +374,23 @@
                 vmem((4, 8, 128), f32),
                 vmem((2, 8, 128), f32),
                 vmem((2, tp_size, 8, 128), f32),
-                dma((2,)), dma((SLOTS,)), dma((4,)),
+                dma((4,)), dma((SLOTS,)), dma((1,)),
                 dma, dma, dma, dma, dma, dma((2,)),
                 dma((2, tp_size)), dma((2, tp_size)),
             ],
             compiler_params=pltpu.CompilerParams(
                 collective_id=0, has_side_effects=True, vmem_limit_bytes=60 * 2**20),
-        )(hidden, draft_ids, temperature, norm_gain.reshape(1, dim), head_shard)
+        )(hidden, draft_ids, temperature, norm_gain, head_shard)
+        return pl.pallas_call(
+            unpack,
+            out_shape=(
+                jax.ShapeDtypeStruct(draft_ids.shape, f32),
+                jax.ShapeDtypeStruct((batch, width), f32),
+                jax.ShapeDtypeStruct((batch, width), f32),
+            ),
+            in_specs=[out],
+            out_specs=(out, out, out),
+        )(pltpu.with_memory_space_constraint(lines, pltpu.VMEM))
 
     return jax.shard_map(
         local_step,

time: 47 us -> 31.8 us (0.68)
  Pallas kernels: 40.9 us -> 31.1 us
  local copies, waits for them, and re-layouts: 5.1 us -> 0 us
    pallas_call x1, Pallas kernels: 40.9 us -> 30.4 us  [local_step(): pl.pallas_call(functools.partial(kernel, tp_size, n_own, n_all, last_rows...]
    unnamed x3 -> x0, local copies, waits for them, and re-layouts: 3.8 us -> none
    reshape x1 -> x0, local copies, waits for them, and re-layouts: 1.3 us -> none  [local_step(): norm_gain.reshape(1, dim)]
    pallas_call x0 -> x1, Pallas kernels: none -> 0.68 us  [local_step(): pl.pallas_call(unpack, out_shape=(jax.ShapeDtypeStruct(draft_ids.shape, f...]
where the time goes in v2:
time: 31.8 us; the launch traced here: 31.7 us
  Pallas kernels  31.1 us (98%)
  between operations  0.64 us (2%)
    pallas_call x1, Pallas kernels, local_step(): pl.pallas_call(functools.partial(kernel, tp_size, n_own, n_all, last_rows...  30.4 us
    pallas_call x1, Pallas kernels, local_step(): pl.pallas_call(unpack, out_shape=(jax.ShapeDtypeStruct(draft_ids.shape, f...  0.68 us

profile of v2, /device:TPU:113, one launch (start us, length us, event | category | flops | bytes accessed | tf_op | source)
XLA Modules:
  0.0 31.7 jit_solution(15184598502504174544)
XLA Ops:
  0.6 30.4 %shard_map.76.lines_ref = f32[8,128]{1,0:T(8,128)S(1)} custom-call(bf16[6,6,3072]{2,1,0:T(8,128)(2,1)} %hidden_hbm.1, s32[6,5]{1,0:T(8,128)} %draft_hbm.1, f32[6]{0:T(128)} %temp_hbm.1, bf16[3072]{0:T(1024)(128)(2,1)} %gain_hbm.1, bf16[16032,3072]{1,0:T(8,128)(2,1)} %w_hbm.1), custom_call_target="tpu_custom_call" | custom-call | tf_op jit(solution)/shard_map/pallas_call | solution.py:356
  31.1 0.7 %shard_map.77 = (f32[6,5]{1,0:T(8,128)}, f32[6,6]{1,0:T(8,128)}, f32[6,6]{1,0:T(8,128)}) custom-call(f32[8,128]{1,0:T(8,128)S(1)} %shard_map.76.lines_ref), custom_call_target="tpu_custom_call" | custom-call | tf_op jit(solution)/shard_map/pallas_call | solution.py:384

commit v3 on v2

v3 whole, which is shorter than its diff:
```python
import functools

import jax
import jax.numpy as jnp
from jax import lax
from jax.experimental import pallas as pl
from jax.experimental.pallas import tpu as pltpu
from jax.sharding import PartitionSpec as P

NORM_EPS = 1e-5
MESH = pl.DeviceIdType.MESH
LOG2E = 1.4426950408889634
LN2 = 0.6931471805599453
LOW = -1e30
CHUNK = 1024
SLOTS = 6
OTHER = 64
PAIRED = True
BLOCKS_OWN = [[2], [3], [4]]
BLOCKS_LATE = [[0], [1], [2], [3], [4], [5]]
OWN_CHUNKS = 3


def kernel(
    tp_size, blocks, n_own, n_all, last_rows, first_rows, share_rows,
    hidden_hbm, draft_hbm, temp_hbm, gain_hbm, w_hbm,
    out_ref,
    draft_ref, temp_ref, hv, gv, gs, gr, g2, buf, zs, vecs, ids_v, vecs_r, stats, msg, inbox,
    in_sem, w_sem, g_send, g_recv, p_send, p_recv, f_send, f_recv, s_send, s_recv,
):
    dp, tp = lax.axis_index("dp"), lax.axis_index("tp")
    half = lax.rem(dp, 2)
    mate = dp + 1 - 2 * half
    core = lax.rem(tp, 2)
    twin = tp + 1 - 2 * core
    shard_rows, dim = w_hbm.shape
    batch, width = hidden_hbm.shape[:2]
    draft_len = draft_hbm.shape[1]
    hd = dim // 2

    def peer(o, other):
        return (mate if other else dp, lax.rem(tp + o, tp_size))

    far_first = sorted(range(tp_size), key=lambda o: -min(o, tp_size - o))
    peers = [(o, True) for o in far_first] if PAIRED else []
    peers += [(o, False) for o in far_first if o]

    own_rows = first_rows[0] + first_rows[1] + n_own * CHUNK
    shared_base = own_rows + half * share_rows if PAIRED else own_rows

    def chunk(j):
        if j == 0:
            return 0, first_rows[0], 0, 0
        if j == 1:
            return first_rows[0], first_rows[1], 0, first_rows[0]
        rows = last_rows if j == n_all - 1 else CHUNK
        early = first_rows[0] + first_rows[1] + (j - 2) * CHUNK
        if j - 2 < n_own:
            return early, rows, (j - 1) % SLOTS, 0
        return shared_base + (j - 2 - n_own) * CHUNK, rows, (j - 1) % SLOTS, 0

    def w_copy(j):
        row, rows, slot, at = chunk(j)
        if not isinstance(row, int):
            row = pl.multiple_of(row, 16)
        return pltpu.make_async_copy(
            w_hbm.at[pl.ds(row, rows)], buf.at[slot, pl.ds(at, rows)], w_sem.at[0 if j == 0 else slot + 1])

    h_copy = pltpu.make_async_copy(hidden_hbm, hv, in_sem.at[0])
    gain_copy = pltpu.make_async_copy(gain_hbm, gv, in_sem.at[1])
    draft_copy = pltpu.make_async_copy(draft_hbm, draft_ref, in_sem.at[2])
    temp_copy = pltpu.make_async_copy(temp_hbm, temp_ref, in_sem.at[3])
    h_copy.start()
    gain_copy.start()
    draft_copy.start()
    temp_copy.start()
    for j in range(SLOTS + 1):
        w_copy(j).start(priority=1)

    barrier = pltpu.get_barrier_semaphore()
    for o, other in peers:
        pl.semaphore_signal(barrier, inc=1, device_id=peer(o, other), device_id_type=MESH)

    draft_copy.wait()
    temp_copy.wait()
    lane = lax.broadcasted_iota(jnp.int32, (1, 128), 1)
    scale = jnp.zeros((1, 128), jnp.float32)
    ids = jnp.full((1, 128), -1, jnp.int32)
    for b in range(batch):
        inside = (lane >= b * width) & (lane < (b + 1) * width)
        scale = jnp.where(inside, temp_ref[b], scale)
        for i in range(draft_len):
            ids = jnp.where(lane == b * width + i, draft_ref[b, i], ids)
    scale = jnp.where(lane < batch * width, LOG2E / jnp.where(scale == 0.0, 1.0, scale), 0.0)
    vecs[...] = jnp.zeros_like(vecs)
    vecs[0:1, :] = scale
    vecs[1:2, :] = ids.astype(jnp.float32)
    ids_v[...] = jnp.broadcast_to(ids, (8, 128))
    stats[0] = jnp.full((8, 128), LOW, jnp.float32)
    stats[1] = jnp.zeros((8, 128), jnp.float32)
    stats[2] = jnp.zeros((8, 128), jnp.float32)
    stats[3] = jnp.zeros((8, 128), jnp.float32)
    g2[...] = jnp.zeros_like(g2)

    h_copy.wait()
    gain_copy.wait()
    gain = gv[...].astype(jnp.float32).reshape(1, dim)
    n_pos, n_k = batch * width, hd // 128

    def place(src, h, row):
        for k in range(n_k):
            ks = pl.ds(pl.multiple_of(h * hd + k * 128, 128), 128)
            g2[row : row + n_pos, ks] = src[h, pl.ds(k, n_pos, stride=n_k), :].astype(jnp.bfloat16)

    for b in range(batch):
        hb = hv[b].astype(jnp.float32)
        mean_sq = jnp.sum(hb * hb, axis=-1, keepdims=True) * (1.0 / dim)
        g = (hb * lax.rsqrt(mean_sq + NORM_EPS) * gain).astype(jnp.bfloat16).astype(jnp.float32)
        for c in range(2):
            for k in range(n_k):
                at = c * hd + k * 128
                gs[c, pl.ds(b * width * n_k + k, width, stride=n_k), :] = g[:, at : at + 128]
    for c in range(2):
        place(gs, c, 0)

    g_copy = pltpu.make_async_remote_copy(
        src_ref=gs.at[core], dst_ref=gr.at[core], send_sem=g_send, recv_sem=g_recv,
        device_id=(mate, tp), device_id_type=MESH)
    p_copy = pltpu.make_async_remote_copy(
        src_ref=vecs, dst_ref=vecs_r, send_sem=p_send, recv_sem=p_recv,
        device_id=(mate, tp), device_id_type=MESH)
    f_copy = pltpu.make_async_remote_copy(
        src_ref=gr.at[core], dst_ref=gr.at[core], send_sem=f_send, recv_sem=f_recv.at[core],
        device_id=(dp, twin), device_id_type=MESH)
    f_wait = pltpu.make_async_remote_copy(
        src_ref=gr.at[1 - core], dst_ref=gr.at[1 - core], send_sem=f_send, recv_sem=f_recv.at[1 - core],
        device_id=(dp, twin), device_id_type=MESH)
    def forward():
        g_copy.wait_recv()
        f_copy.start()

    def join(h):
        place(gr, h, OTHER)

    def join_lanes():
        p_copy.wait_recv()
        theirs = lane >= OTHER
        v = pltpu.roll(vecs_r[...], OTHER, 1)
        scale_all[...] = jnp.where(theirs, v[0:1], scale_all[...])
        ids_v[...] = jnp.where(theirs, jnp.broadcast_to(v[1:2].astype(jnp.int32), (8, 128)), ids_v[...])
        stats[0] = jnp.where(theirs, LOW, stats[0])
        for r in range(1, 4):
            stats[r] = jnp.where(theirs, 0.0, stats[r])

    scale_all = msg.at[1]
    scale_all[...] = jnp.broadcast_to(scale, (8, 128))

    def epilogue(z, base):
        rows = z.shape[0]
        z = z.reshape(rows // 8, 8, 128) * scale_all[...][None]
        old = stats[0]
        new = jnp.maximum(old, jnp.max(z, axis=0))
        e = jnp.exp2(z - new[None])
        fix = jnp.exp2(old - new)
        stats[0] = new
        stats[1] = stats[1] * fix + jnp.sum(e, axis=0)
        stats[2] = stats[2] * fix + jnp.sum(e * z, axis=0)
        row = lax.broadcasted_iota(jnp.int32, z.shape, 0) * 8 + lax.broadcasted_iota(jnp.int32, z.shape, 1)
        hit = row == (ids_v[...] - (tp * shard_rows + base))[None]
        stats[3] = stats[3] + jnp.sum(jnp.where(hit, z, 0.0), axis=0)

    def product(j):
        _, rows, slot, at = chunk(j)
        part = rows // 2
        return [
            lax.dot_general(
                buf[slot, at + q * part : at + (q + 1) * part], g2[...],
                (((1,), (1,)), ((), ())), preferred_element_type=jnp.float32)
            for q in range(2)
        ]

    def half_product(j, h):
        _, rows, slot, at = chunk(j)
        part = rows // 2
        ks = pl.ds(pl.multiple_of(h * hd, 128), hd)
        return [
            lax.dot_general(
                buf[slot, pl.ds(at + q * part, part), ks], g2[:, ks],
                (((1,), (1,)), ((), ())), preferred_element_type=jnp.float32)
            for q in range(2)
        ]

    def drain(done):
        for j, z in done:
            base, rows = chunk(j)[:2]
            part = rows // 2
            for q in range(2):
                epilogue(zs[z, q * part : (q + 1) * part], base + q * part)

    done = []
    for n, block in enumerate(blocks):
        forwarding = PAIRED and block[0] == n_own + 1
        joining = PAIRED and block[0] == n_own + 2
        if joining:
            join(core)
        for j in block:
            w_copy(j).wait()
        if n == 0:
            pl.semaphore_wait(barrier, len(peers))
            if PAIRED:
                g_copy.start()
                p_copy.start()
        if forwarding or joining:
            first = half_product(block[0], core)
            if forwarding:
                z = 2 * (n % 2)
                for q in range(2):
                    zs[z, q * (CHUNK // 2) : (q + 1) * (CHUNK // 2)] = first[q]
                forward()
                second = half_product(block[0], 1 - core)
                first = [zs[z, q * (CHUNK // 2) : (q + 1) * (CHUNK // 2)] for q in range(2)]
            else:
                drain(done)
                done = []
                z = 2 * (n % 2)
                for q in range(2):
                    zs[z, q * (CHUNK // 2) : (q + 1) * (CHUNK // 2)] = first[q]
                f_wait.wait_recv()
                join(1 - core)
                second = half_product(block[0], 1 - core)
                first = [zs[z, q * (CHUNK // 2) : (q + 1) * (CHUNK // 2)] for q in range(2)]
            parts = [[x + y for x, y in zip(first, second)]]
        else:
            parts = [product(j) for j in block]
        drain(done)
        done = [(j, 2 * (n % 2) + i) for i, j in enumerate(block)]
        for (j, z), p in zip(done, parts):
            rows = p[0].shape[0]
            for q in range(2):
                zs[z, q * rows : (q + 1) * rows] = p[q]
        if joining:
            join_lanes()
        for j in block:
            if 1 <= j and j + SLOTS < n_all:
                w_copy(j + SLOTS).start(priority=1)
    drain(done)

    m8 = stats[0]
    m1 = jnp.max(m8, axis=0, keepdims=True)
    w8 = jnp.exp2(m8 - m1)
    out = msg.at[0]
    out[4:8, :] = jnp.zeros((4, 128), jnp.float32)
    out[0:1, :] = m1
    out[1:2, :] = jnp.sum(stats[1] * w8, axis=0, keepdims=True)
    out[2:3, :] = jnp.sum(stats[2] * w8, axis=0, keepdims=True)
    out[3:4, :] = jnp.sum(stats[3], axis=0, keepdims=True)

    def s_copy(o, other, source):
        i = 1 if other else 0
        return pltpu.make_async_remote_copy(
            src_ref=msg.at[0], dst_ref=inbox.at[i * tp_size + source], send_sem=s_send, recv_sem=s_recv,
            device_id=peer(o, other), device_id_type=MESH)

    for o, other in peers:
        s_copy(o, other, tp).start()
    inbox[tp] = msg[0]
    others = inbox.at[pl.ds(0, len(peers))]
    everything = pltpu.make_async_remote_copy(
        src_ref=others, dst_ref=others, send_sem=s_send, recv_sem=s_recv,
        device_id=peer(1, False), device_id_type=MESH)
    everything.wait_recv()

    def combine(x):
        m = jnp.max(x[:, 0:1, :], axis=0)
        r = lax.broadcasted_iota(jnp.int32, x.shape, 1)
        weight = jnp.exp2(x[:, 0:1, :] - m[None])
        s = jnp.sum(jnp.where((r == 1) | (r == 2), x * weight, x), axis=0)
        return m, s

    m, s = combine(inbox[0:tp_size])
    if PAIRED:
        m2, s2 = combine(inbox[tp_size:])
        m2 = pltpu.roll(jnp.broadcast_to(m2, (8, 128)), OTHER, 1)[0:1]
        s2 = pltpu.roll(s2, OTHER, 1)
        top = jnp.maximum(m, m2)
        r = lax.broadcasted_iota(jnp.int32, s.shape, 0)
        ours, theirs = jnp.exp2(m - top), jnp.exp2(m2 - top)
        scaled = (r == 1) | (r == 2)
        s = jnp.where(scaled, s * ours, s) + jnp.where(scaled, s2 * theirs, s2)
        m = top
    lse = m * LN2 + jnp.log(s[1:2])
    ent = lse - LN2 * (s[2:3] / s[1:2])
    lp = LN2 * s[3:4] - lse

    if PAIRED:
        p_copy.wait_send()
    vecs[0:1, :] = lse
    vecs[1:2, :] = ent
    vecs[2:3, :] = lp
    out_ref[...] = vecs[...]

    everything.wait_send()
    if PAIRED:
        g_copy.wait_send()
        f_copy.wait_send()


def unpack(lines_ref, lp_ref, lse_ref, ent_ref):
    batch, width = lse_ref.shape
    for b in range(batch):
        line = pltpu.roll(lines_ref[...], (128 - b * width) % 128, 1)
        lse_ref[b : b + 1, :] = line[0:1, :width]
        ent_ref[b : b + 1, :] = line[1:2, :width]
        lp_ref[b : b + 1, :] = line[2:3, : lp_ref.shape[1]]


def solution(mesh):
    tp_size = mesh.shape["tp"]

    def local_step(hidden, draft_ids, temperature, norm_gain, head_shard):
        batch, width, dim = hidden.shape
        shard_rows = head_shard.shape[0]
        short = shard_rows % CHUNK
        first_rows = (short // 3, short - short // 3)
        n_own = OWN_CHUNKS
        share_rows = (shard_rows - short - n_own * CHUNK) // 2
        n_late = -(-share_rows // CHUNK)
        last_rows = share_rows - (n_late - 1) * CHUNK
        n_all = 2 + n_own + n_late
        late = n_own + 2
        blocks = [[0], [1]] + BLOCKS_OWN + [[late + i for i in x] for x in BLOCKS_LATE]
        vmem, dma = pltpu.VMEM, pltpu.SemaphoreType.DMA
        f32, bf16 = jnp.float32, jnp.bfloat16
        any_space = pl.BlockSpec(memory_space=pltpu.HBM)
        out = pl.BlockSpec(memory_space=pltpu.VMEM)
        lines = pl.pallas_call(
            functools.partial(kernel, tp_size, blocks, n_own, n_all, last_rows, first_rows, share_rows),
            out_shape=pltpu.VMEM((8, 128), f32),
            in_specs=[any_space] * 5,
            out_specs=out,
            scratch_shapes=[
                pltpu.SMEM(draft_ids.shape, jnp.int32),
                pltpu.SMEM(temperature.shape, f32),
                vmem(hidden.shape, bf16),
                vmem((dim,), bf16),
                vmem((2, batch * width * (dim // 256), 128), f32),
                vmem((2, batch * width * (dim // 256), 128), f32),
                vmem((128, dim), bf16),
                vmem((SLOTS, CHUNK, dim), bf16),
                vmem((4, CHUNK, 128), f32),
                vmem((8, 128), f32),
                vmem((8, 128), jnp.int32),
                vmem((8, 128), f32),
                vmem((4, 8, 128), f32),
                vmem((2, 8, 128), f32),
                vmem((2 * tp_size, 8, 128), f32),
                dma((4,)), dma((SLOTS + 1,)),
                dma, dma, dma, dma, dma, dma((2,)),
                dma, dma,
            ],
            compiler_params=pltpu.CompilerParams(
                collective_id=0, has_side_effects=True, vmem_limit_bytes=60 * 2**20),
        )(hidden, draft_ids, temperature, norm_gain, head_shard)
        return pl.pallas_call(
            unpack,
            out_shape=(
                jax.ShapeDtypeStruct(draft_ids.shape, f32),
                jax.ShapeDtypeStruct((batch, width), f32),
                jax.ShapeDtypeStruct((batch, width), f32),
            ),
            in_specs=[out],
            out_specs=(out, out, out),
        )(pltpu.with_memory_space_constraint(lines, pltpu.VMEM))

    return jax.shard_map(
        local_step,
        mesh=mesh,
        in_specs=(P("dp", None, None), P("dp", None), P("dp"), P(None), P("tp", None)),
        out_specs=(P("dp", None), P("dp", None), P("dp", None)),
        check_vma=False,
    )
```

time: 31.8 us -> 30.3 us (0.953)
  Pallas kernels: 31.1 us -> 29.5 us
    pallas_call x1, Pallas kernels: 30.4 us -> 28.9 us  [local_step(): pl.pallas_call(functools.partial(kernel, tp_size, blocks, n_own, n_all, l...]
where the time goes in v3:
time: 30.3 us; the launch traced here: 30.2 us
  Pallas kernels  29.5 us (97%)
  between operations  0.64 us (2%)
    pallas_call x1, Pallas kernels, local_step(): pl.pallas_call(functools.partial(kernel, tp_size, blocks, n_own, n_all, l...  28.9 us
    pallas_call x1, Pallas kernels, local_step(): pl.pallas_call(unpack, out_shape=(jax.ShapeDtypeStruct(draft_ids.shape, f...  0.68 us

profile of v3, /device:TPU:113, one launch (start us, length us, event | category | flops | bytes accessed | tf_op | source)
XLA Modules:
  0.0 30.2 jit_solution(4945574882837169290)
XLA Ops:
  0.6 28.9 %shard_map.76.lines_ref = f32[8,128]{1,0:T(8,128)S(1)} custom-call(bf16[6,6,3072]{2,1,0:T(8,128)(2,1)} %hidden_hbm.1, s32[6,5]{1,0:T(8,128)} %draft_hbm.1, f32[6]{0:T(128)} %temp_hbm.1, bf16[3072]{0:T(1024)(128)(2,1)} %gain_hbm.1, bf16[16032,3072]{1,0:T(8,128)(2,1)} %w_hbm.1), custom_call_target="tpu_custom_call" | custom-call | tf_op jit(solution)/shard_map/pallas_call | solution.py:336
  29.5 0.7 %shard_map.77 = (f32[6,5]{1,0:T(8,128)}, f32[6,6]{1,0:T(8,128)}, f32[6,6]{1,0:T(8,128)}) custom-call(f32[8,128]{1,0:T(8,128)S(1)} %shard_map.76.lines_ref), custom_call_target="tpu_custom_call" | custom-call | tf_op jit(solution)/shard_map/pallas_call | solution.py:364

commit v4 on v3

--- a/solution.py
+++ b/solution.py
@@ -9,9 +9,7 @@
 
 NORM_EPS = 1e-5
 MESH = pl.DeviceIdType.MESH
-LOG2E = 1.4426950408889634
-LN2 = 0.6931471805599453
-LOW = -1e30
+LOW = -3.4e38
 CHUNK = 1024
 SLOTS = 6
 OTHER = 64
@@ -91,7 +89,7 @@
         scale = jnp.where(inside, temp_ref[b], scale)
         for i in range(draft_len):
             ids = jnp.where(lane == b * width + i, draft_ref[b, i], ids)
-    scale = jnp.where(lane < batch * width, LOG2E / jnp.where(scale == 0.0, 1.0, scale), 0.0)
+    scale = jnp.where(lane < batch * width, 1.0 / jnp.where(scale == 0.0, 1.0, scale), 0.0)
     vecs[...] = jnp.zeros_like(vecs)
     vecs[0:1, :] = scale
     vecs[1:2, :] = ids.astype(jnp.float32)
@@ -160,8 +158,8 @@
         z = z.reshape(rows // 8, 8, 128) * scale_all[...][None]
         old = stats[0]
         new = jnp.maximum(old, jnp.max(z, axis=0))
-        e = jnp.exp2(z - new[None])
-        fix = jnp.exp2(old - new)
+        e = jnp.exp(z - new[None])
+        fix = jnp.exp(old - new)
         stats[0] = new
         stats[1] = stats[1] * fix + jnp.sum(e, axis=0)
         stats[2] = stats[2] * fix + jnp.sum(e * z, axis=0)
@@ -247,7 +245,7 @@
 
     m8 = stats[0]
     m1 = jnp.max(m8, axis=0, keepdims=True)
-    w8 = jnp.exp2(m8 - m1)
+    w8 = jnp.exp(m8 - m1)
     out = msg.at[0]
     out[4:8, :] = jnp.zeros((4, 128), jnp.float32)
     out[0:1, :] = m1
@@ -273,7 +271,7 @@
     def combine(x):
         m = jnp.max(x[:, 0:1, :], axis=0)
         r = lax.broadcasted_iota(jnp.int32, x.shape, 1)
-        weight = jnp.exp2(x[:, 0:1, :] - m[None])
+        weight = jnp.exp(x[:, 0:1, :] - m[None])
         s = jnp.sum(jnp.where((r == 1) | (r == 2), x * weight, x), axis=0)
         return m, s
 
@@ -284,13 +282,13 @@
         s2 = pltpu.roll(s2, OTHER, 1)
         top = jnp.maximum(m, m2)
         r = lax.broadcasted_iota(jnp.int32, s.shape, 0)
-        ours, theirs = jnp.exp2(m - top), jnp.exp2(m2 - top)
+        ours, theirs = jnp.exp(m - top), jnp.exp(m2 - top)
         scaled = (r == 1) | (r == 2)
         s = jnp.where(scaled, s * ours, s) + jnp.where(scaled, s2 * theirs, s2)
         m = top
-    lse = m * LN2 + jnp.log(s[1:2])
-    ent = lse - LN2 * (s[2:3] / s[1:2])
-    lp = LN2 * s[3:4] - lse
+    lse = m + jnp.log(s[1:2])
+    ent = lse - (s[2:3] / s[1:2])
+    lp = s[3:4] - lse
 
     if PAIRED:
         p_copy.wait_send()

time: 30.3 us -> 30.7 us (1.013)
  Pallas kernels: 29.5 us -> 30 us
    pallas_call x1, Pallas kernels: 28.9 us -> 29.4 us  [local_step(): pl.pallas_call(functools.partial(kernel, tp_size, blocks, n_own, n_all, l...]
where the time goes in v4:
time: 30.7 us
  Pallas kernels  30 us (98%)
  between operations  0.64 us (2%)
    pallas_call x1, Pallas kernels, local_step(): pl.pallas_call(functools.partial(kernel, tp_size, blocks, n_own, n_all, l...  29.4 us
    pallas_call x1, Pallas kernels, local_step(): pl.pallas_call(unpack, out_shape=(jax.ShapeDtypeStruct(draft_ids.shape, f...  0.68 us

profile of v4, /device:TPU:113, one launch (start us, length us, event | category | flops | bytes accessed | tf_op | source)
XLA Modules:
  0.0 30.7 jit_solution(6661452077913726392)
XLA Ops:
  0.6 29.4 %shard_map.76.lines_ref = f32[8,128]{1,0:T(8,128)S(1)} custom-call(bf16[6,6,3072]{2,1,0:T(8,128)(2,1)} %hidden_hbm.1, s32[6,5]{1,0:T(8,128)} %draft_hbm.1, f32[6]{0:T(128)} %temp_hbm.1, bf16[3072]{0:T(1024)(128)(2,1)} %gain_hbm.1, bf16[16032,3072]{1,0:T(8,128)(2,1)} %w_hbm.1), custom_call_target="tpu_custom_call" | custom-call | tf_op jit(solution)/shard_map/pallas_call | solution.py:334
  30.0 0.7 %shard_map.77 = (f32[6,5]{1,0:T(8,128)}, f32[6,6]{1,0:T(8,128)}, f32[6,6]{1,0:T(8,128)}) custom-call(f32[8,128]{1,0:T(8,128)S(1)} %shard_map.76.lines_ref), custom_call_target="tpu_custom_call" | custom-call | tf_op jit(solution)/shard_map/pallas_call | solution.py:362
